TPU v7x, 256 devices: a whole 4x4x8 slice. The times are simulated.
256 devices in a mesh: orb: 4 (over y), grid: 64 (over z, x, core).
Axes of the slice: x: 4, y: 4, z: 8, core: 2. Of those that a mesh axis runs over, the one named last changes fastest.
Arguments:
- orbitals: float32 [256, 2048, 128], P('orb', 'grid'), may hold values from -6 to 6
- previous: float32 [256, 2048, 128], P('orb', 'grid'), may hold values from -6 to 6
- potential: float32 [256, 2048, 128], P('orb', 'grid'), may hold values from -3 to 3
- partners: int32 [256, 3], P(('orb', 'grid')), may hold values from 0 to 255, as said below
- offsets: int32 [256, 3, 3], P(('orb', 'grid')), may hold values from -16 to 16, as said below
Outputs:
- advanced: float32 [256, 2048, 128], P('orb', 'grid')
- exchange_force: float32 [256, 2048, 128], P('orb', 'grid')
Inputs may be any that keep to these rules, and one draw needn't show every extreme that they name: `partners`: row n names three different orbitals among n + 1 to n + 4, counted modulo 256; so every intersecting pair is listed once, by its first orbital. There are integer box corners of the orbitals with offsets[n, q, :] = corner[partners[n, q]] - corner[n]; both ends of the range occur in every draw.
All inputs are finite; a program needn't handle non-finite values.
Results may differ from a plain program's by a relative error of at most 0.0003.
Values sent between devices are 32-bit elements; how exact they have to be, the bound alone decides.
No kernel may reach another device: no remote copies, remote signals or barrier semaphores. Data moves between devices by JAX's collectives and lax.ppermute only.
A program may use at most 128 MiB of HBM per device.

v0:
```python
import math
import jax
import jax.numpy as jnp
from jax import lax
from jax.sharding import Mesh
from jax.sharding import PartitionSpec as P

B = 64
SWEEPS = 4
AHEAD = 4
GRID = ("grid_0", "grid_1", "grid_2")
ORB_GRID = ("orb", "grid_0", "grid_1", "grid_2")
coulomb_factor = 4.0 * math.pi
exact_share = 0.25
verlet_factor = 0.05
lower_edge = 0.5
upper_edge = 16.0


def from_behind(array, axis, by):
    count = lax.axis_size(axis)
    return lax.ppermute(array, axis, [(i, (i + by) % count) for i in range(count)])


def cut_along(array, dim, count):
    before, after = (array.shape[:dim], array.shape[dim + 1 :])
    return jnp.moveaxis(array.reshape(*before, count, -1, *after), dim, 0)


def joined_along(blocks, dim):
    blocks = jnp.moveaxis(blocks, 0, dim)
    lengths = blocks.shape
    return blocks.reshape(*lengths[:dim], lengths[dim] * lengths[dim + 1], *lengths[dim + 2 :])


def exchange_in_order(blocks, axes, sequence):
    inside = blocks.shape[1:]
    out = blocks.reshape(*(lax.axis_size(a) for a in axes), *inside)
    for k in sequence:
        out = lax.all_to_all(out, axes[k], k, k, tiled=True)
    return out.reshape(-1, *inside)


def two_step_exchange(array, groups, sequence, split_dim, concat_dim):
    count = lax.axis_size(groups[0]) * lax.axis_size(groups[1])
    blocks = cut_along(array, split_dim, count)
    return joined_along(exchange_in_order(blocks, groups, sequence), concat_dim)


def apply_operator(grid_field):
    leading = grid_field.ndim - 3
    padded = jnp.pad(grid_field, [(0, 0)] * leading + [(2, 2)] * 3)
    extent = grid_field.shape[-1]

    def displaced(axis_number, offset_cells):
        corner = [2, 2, 2]
        corner[axis_number] = 2 + offset_cells
        return padded[
            ...,
            corner[0] : corner[0] + extent,
            corner[1] : corner[1] + extent,
            corner[2] : corner[2] + extent,
        ]

    nearest = (
        displaced(0, 1)
        + displaced(0, -1)
        + displaced(1, 1)
        + displaced(1, -1)
        + displaced(2, 1)
        + displaced(2, -1)
    )
    farther = (
        displaced(0, 2)
        + displaced(0, -2)
        + displaced(1, 2)
        + displaced(1, -2)
        + displaced(2, 2)
        + displaced(2, -2)
    )
    return 7.5 * grid_field - 4.0 / 3.0 * nearest + 1.0 / 12.0 * farther


def sweep_weights():
    centre = 0.5 * (upper_edge + lower_edge)
    radius = 0.5 * (upper_edge - lower_edge)
    ratio_sigma = centre / radius
    previous_rho = 1.0 / ratio_sigma
    weights = []
    for turn_index in range(SWEEPS - 1):
        current_rho = 1.0 / (2.0 * ratio_sigma - previous_rho)
        weights.append((current_rho * previous_rho, 2.0 * current_rho / radius))
        previous_rho = current_rho
    return (centre, weights)


def solve_potential(density):
    centre, weights = sweep_weights()
    residual = coulomb_factor * density
    direction = residual / centre
    solution = jnp.zeros_like(density)
    for turn_index in range(SWEEPS):
        solution = solution + direction
        residual = residual - apply_operator(direction)
        if turn_index + 1 < SWEEPS:
            keep_weight, residual_weight = weights[turn_index]
            direction = keep_weight * direction + residual_weight * residual
    return solution


def shift_box(one_box, offset, direction_sign):
    extent = one_box.shape[0]
    reach_cells = extent // 4
    padded = jnp.pad(one_box, reach_cells)
    corner = (reach_cells + direction_sign * offset).astype(jnp.int32)
    return lax.dynamic_slice(padded, (corner[0], corner[1], corner[2]), (extent, extent, extent))


def pair_terms(own_box, partner_boxes, pair_offsets):

    def single(partner_box, offset):
        moved_box = shift_box(partner_box, offset, 1)
        potential_box = solve_potential(own_box * moved_box)
        return (potential_box * moved_box, shift_box(potential_box * own_box, offset, -1))

    own_terms, partner_terms = jax.vmap(single)(partner_boxes, pair_offsets)
    return (jnp.sum(own_terms, axis=0), partner_terms)


def build_windows(orbitals, upper_rows, count_local, steps_ahead):
    slab_count = lax.axis_size(GRID)
    tail_shape = orbitals.shape[1:]
    blocks = jnp.concatenate([orbitals, upper_rows], axis=0)
    blocks = blocks.reshape((slab_count + steps_ahead, count_local) + tail_shape)
    ahead_rows = jnp.concatenate(
        [blocks[distance + 1 : distance + 1 + slab_count] for distance in range(steps_ahead)],
        axis=1,
    )
    windows = jnp.concatenate([blocks[:slab_count], ahead_rows], axis=1)
    return windows.reshape((slab_count * (count_local + AHEAD),) + tail_shape)


def fold_windows(returned, count_local, steps_ahead):
    slab_count = lax.axis_size(GRID)
    tail_shape = returned.shape[1:]
    blocks = returned.reshape((slab_count, count_local + AHEAD) + tail_shape)
    ahead_rows = blocks[:, count_local:]
    summed = jnp.pad(blocks[:, :count_local], ((0, steps_ahead), (0, 0), (0, 0), (0, 0)))
    for distance in range(steps_ahead):
        ahead_part = ahead_rows[:, distance * count_local : (distance + 1) * count_local]
        summed = summed + jnp.pad(
            ahead_part, ((distance + 1, steps_ahead - distance - 1), (0, 0), (0, 0), (0, 0))
        )
    flattened = summed.reshape(((slab_count + steps_ahead) * count_local,) + tail_shape)
    kept_rows = slab_count * count_local
    spilled = from_behind(flattened[kept_rows : kept_rows + AHEAD], "orb", 1)
    return flattened[:kept_rows] + jnp.pad(spilled, ((0, kept_rows - AHEAD), (0, 0), (0, 0)))


def local(orbitals, previous, potential, partners, offsets):
    count_local = partners.shape[0]
    width_last = orbitals.shape[2]
    total_orbitals = lax.axis_size(ORB_GRID) * count_local
    steps_ahead = -(-AHEAD // count_local)
    upper_rows = from_behind(orbitals[:AHEAD], "orb", -1)
    windows = build_windows(orbitals, upper_rows, count_local, steps_ahead)
    widened = lax.all_to_all(windows, GRID, split_axis=0, concat_axis=1, tiled=True)
    full_rows = widened.shape[1]
    extended = widened.reshape(count_local + AHEAD, B, B, B)
    own_boxes = extended[:count_local]
    first_index = lax.axis_index(ORB_GRID) * count_local
    local_index = jnp.remainder(partners - first_index, total_orbitals)

    def per_orbital(packed):
        own_box, chosen, pair_offsets = packed
        return pair_terms(own_box, extended[chosen], pair_offsets)

    own_force, partner_force = lax.map(per_orbital, (own_boxes, local_index, offsets))
    spread = (
        jnp.zeros_like(extended)
        .at[local_index.reshape(-1)]
        .add(partner_force.reshape((-1,) + extended.shape[1:]))
    )
    kinetic = (-0.5 * apply_operator(own_boxes)).reshape(count_local, full_rows, width_last)
    all_force = jnp.concatenate([own_force + spread[:count_local], spread[count_local:]], axis=0)
    packed_all = (exact_share * all_force).reshape(count_local + AHEAD, full_rows, width_last)
    returned, restored = (
        two_step_exchange(packed_all, (("grid_0", "grid_1"), "grid_2"), (0, 1), 1, 0),
        two_step_exchange(kinetic, (("grid_0", "grid_1"), "grid_2"), (0, 1), 1, 0),
    )
    exchange_force = fold_windows(returned, count_local, steps_ahead)
    advanced = (
        2.0 * orbitals
        - previous
        + verlet_factor * (restored + exchange_force - potential * orbitals)
    )
    return (advanced, exchange_force)


def solution(mesh):
    split = Mesh(
        mesh.devices.reshape(mesh.shape["orb"], 8, 4, 2), ("orb", "grid_0", "grid_1", "grid_2")
    )
    return jax.shard_map(
        local,
        mesh=split,
        in_specs=(
            P("orb", GRID, None),
            P("orb", GRID, None),
            P("orb", GRID, None),
            P(ORB_GRID, None),
            P(ORB_GRID, None, None),
        ),
        out_specs=(P("orb", GRID, None), P("orb", GRID, None)),
        check_vma=False,
    )
```

profile of v0, /device:TPU:2, one launch (start us, length us, event | category | flops | bytes accessed | tf_op | source)
XLA Modules:
  0.0 577.9 jit_solution(16364896627483350653)
XLA Ops:
  9.8 12.2 %all-to-all-start = ((f32[320,32,128]{2,1,0:T(8,128)}), f32[320,32,128]{2,1,0:T(8,128)}, u32[]{:S(2)}, u32[]{:S(2)}) async-start(f32[320,32,128]{2,1,0:T(8,128)} %bitcast.114), calls=%async_computation | async-start | bytes 10485760 | tf_op jit(solution)/shard_map/all_to_all | solution.py:167
  22.4 118.1 %all-to-all-done = f32[320,32,128]{2,1,0:T(8,128)} async-done(((f32[320,32,128]{2,1,0:T(8,128)}), f32[320,32,128]{2,1,0:T(8,128)}, u32[]{:S(2)}, u32[]{:S(2)}) %all-to-all-start) | async-done | bytes 5242912 | tf_op jit(solution)/shard_map/all_to_all | solution.py:167
  140.6 8.5 %reshape.78 = f32[5,64,64,64]{3,2,0,1:T(8,128)} reshape(f32[5,64,32,128]{3,2,0,1:T(8,128)} %bitcast.10) | data formatting | bytes 10485760 | tf_op jit(solution)/shard_map/reshape | solution.py:169
  152.4 7.5 %gather_fusion = f32[3,64,64,64]{3,2,1,0:T(8,128)} fusion(f32[5,64,64,64]{3,2,0,1:T(8,128)} %reshape.78, s32[1024]{0:T(1024)S(1)} %pad_clamp_fusion), kind=kCustom, calls=%fused_computation | custom fusion | bytes 6291468 | tf_op jit(solution)/shard_map/while/body/eval_jaxpr/gather | solution.py:176
  159.9 10.5 %pad.51 = f32[3,96,96,96]{3,2,1,0:T(8,128)} pad(f32[3,64,64,64]{3,2,1,0:T(8,128)} %gather_fusion, f32[]{:T(128)} %constant.49.clone.1), padding=0_0x16_16x16_16x16_16 | pad | bytes 13762564 | tf_op jit(solution)/shard_map/while/body/eval_jaxpr/vmap(jit(_pad))/pad | solution.py:114
  170.4 3.5 broadcast.154.clone
  173.9 20.5 %while.2 = (s32[]{:T(128)}, f32[3,96,96,96]{3,2,1,0:T(8,128)}, s32[3,4]{1,0:T(4,128)S(1)}, f32[3,64,64,64]{3,2,1,0:T(8,128)}, s32[]{:T(128)}) while((s32[]{:T(128)}, f32[3,96,96,96]{3,2,1,0:T(8,128)}, s32[3,4]{1,0:T(4,128)S(1)}, f32[3,64,64,64]{3,2,1,0:T(8,128)}, s32[]{:T(128)}) %tuple.70), condition=%wide.while_cond, body=%wide.while_body.sunk | while | flops 2 | bytes 4196993 | solution.py:116
  174.6 6.2 %dynamic-slice_dynamic-update-slice_fusion.4 = f32[3,64,64,64]{3,2,1,0:T(8,128)} fusion(f32[3,64,64,64]{3,2,1,0:T(8,128)} %get-tuple-element.203, s32[]{:T(128)} %get-tuple-element.200, f32[3,96,96,96]{3,2,1,0:T(8,128)} %get-tuple-element.206, s32[]{:T(128)} %bitcast.104, s32[]{:T(128)} %bitcast.105, s32[]{:T(128)} %bitcast.106, s32[]{:T(128)} %bitcast.107), kind=kLoop, calls=%fused_computation.2.clone.1 | loop fusion | bytes 4196864 | tf_op jit(solution)/shard_map/while/body/eval_jaxpr/vmap()/gather
  181.5 6.1 %dynamic-slice_dynamic-update-slice_fusion.4 = f32[3,64,64,64]{3,2,1,0:T(8,128)} fusion(f32[3,64,64,64]{3,2,1,0:T(8,128)} %get-tuple-element.203, s32[]{:T(128)} %get-tuple-element.200, f32[3,96,96,96]{3,2,1,0:T(8,128)} %get-tuple-element.206, s32[]{:T(128)} %bitcast.104, s32[]{:T(128)} %bitcast.105, s32[]{:T(128)} %bitcast.106, s32[]{:T(128)} %bitcast.107), kind=kLoop, calls=%fused_computation.2.clone.1 | loop fusion | bytes 4196864 | tf_op jit(solution)/shard_map/while/body/eval_jaxpr/vmap()/gather
  188.3 6.2 %dynamic-slice_dynamic-update-slice_fusion.4 = f32[3,64,64,64]{3,2,1,0:T(8,128)} fusion(f32[3,64,64,64]{3,2,1,0:T(8,128)} %get-tuple-element.203, s32[]{:T(128)} %get-tuple-element.200, f32[3,96,96,96]{3,2,1,0:T(8,128)} %get-tuple-element.206, s32[]{:T(128)} %bitcast.104, s32[]{:T(128)} %bitcast.105, s32[]{:T(128)} %bitcast.106, s32[]{:T(128)} %bitcast.107), kind=kLoop, calls=%fused_computation.2.clone.1 | loop fusion | bytes 4196864 | tf_op jit(solution)/shard_map/while/body/eval_jaxpr/vmap()/gather
  194.5 6.9 %multiply_multiply_fusion = f32[3,64,64,64]{3,2,1,0:T(8,128)} fusion(f32[3,64,64,64]{3,2,1,0:T(8,128)} %get-tuple-element.30, f32[64,64,64]{2,1,0:T(8,128)S(1)} %mul.171), kind=kLoop, calls=%fused_computation.93 | loop fusion | flops 1572864 | bytes 7340032 | tf_op jit(solution)/shard_map/while/body/eval_jaxpr/vmap()/div | solution.py:100
  201.3 35.3 %multiply_add_fusion.1 = (f32[3,64,64,64]{3,2,1,0:T(8,128)}, f32[3,64,64,64]{3,2,1,0:T(8,128)}) fusion(f32[3,64,64,64]{3,2,1,0:T(8,128)} %get-tuple-element.30, f32[64,64,64]{2,1,0:T(8,128)S(1)} %mul.171, f32[3,64,64,64]{3,2,1,0:T(8,128)} %multiply_multiply_fusion), kind=kLoop, calls=%fused_computation.92 | loop fusion | flops 16515072 | bytes 13631488 | tf_op jit(solution)/shard_map/while/body/eval_jaxpr/vmap()/add | solution.py:107
  236.6 15.6 %fusion.56 = f32[1,64,64,64]{3,2,1,0:T(8,128)} fusion(f32[1,64,64,64]{3,2,1,0:T(8,128)} %slice.290), kind=kLoop, calls=%fused_computation.116 | loop fusion | flops 4194304 | bytes 2097152 | tf_op jit(solution)/shard_map/mul | solution.py:184
  254.8 5.1 all-to-all-start.1
  259.9 35.4 %multiply_add_fusion = (f32[3,64,64,64]{3,2,1,0:T(8,128)}, f32[3,64,64,64]{3,2,1,0:T(8,128)}) fusion(f32[3,64,64,64]{3,2,1,0:T(8,128)} %get-tuple-element.101, f32[3,64,64,64]{3,2,1,0:T(8,128)} %get-tuple-element.102), kind=kLoop, calls=%fused_computation.91 | loop fusion | flops 14942208 | bytes 12582912 | tf_op jit(solution)/shard_map/while/body/eval_jaxpr/vmap()/add | solution.py:107
  295.3 42.7 %multiply_reduce_fusion = (f32[64,64,64]{2,1,0:T(8,128)}, f32[3,64,64,64]{3,2,1,0:T(8,128)}) fusion(f32[3,64,64,64]{3,2,1,0:T(8,128)} %get-tuple-element.30, f32[3,64,64,64]{3,2,1,0:T(8,128)} %get-tuple-element.100, f32[3,64,64,64]{3,2,1,0:T(8,128)} %get-tuple-element.99, f32[3,64,64,64]{3,2,1,0:T(8,128)} %get-tuple-element.101, f32[64,64,64]{2,1,0:T(8,128)S(1)} %mul.171), kind=kLoop, calls=%fused_computation.90 | loop fusion | flops 20185088 | bytes 17825792 | tf_op jit(solution)/shard_map/while/body/eval_jaxpr/reduce_sum | solution.py:127
  338.0 6.8 %broadcast_multiply_fusion = f32[3,64,64,64]{3,2,1,0:T(8,128)} fusion(f32[3,64,64,64]{3,2,1,0:T(8,128)} %get-tuple-element.98, f32[64,64,64]{2,1,0:T(8,128)S(1)} %mul.171), kind=kLoop, calls=%fused_computation.95 | loop fusion | flops 786432 | bytes 7340032 | tf_op jit(solution)/shard_map/while/body/eval_jaxpr/vmap()/mul | solution.py:124
  344.7 10.5 %pad.55 = f32[3,96,96,96]{3,2,1,0:T(8,128)} pad(f32[3,64,64,64]{3,2,1,0:T(8,128)} %broadcast_multiply_fusion, f32[]{:T(128)} %constant.49.clone.1), padding=0_0x16_16x16_16x16_16 | pad | bytes 13762564 | tf_op jit(solution)/shard_map/while/body/eval_jaxpr/vmap(jit(_pad))/pad | solution.py:114
  355.2 3.4 broadcast.154
  358.6 20.2 %while.3 = (s32[]{:T(128)}, f32[3,96,96,96]{3,2,1,0:T(8,128)}, s32[3,4]{1,0:T(4,128)S(1)}, f32[3,64,64,64]{3,2,1,0:T(8,128)}, s32[]{:T(128)}) while((s32[]{:T(128)}, f32[3,96,96,96]{3,2,1,0:T(8,128)}, s32[3,4]{1,0:T(4,128)S(1)}, f32[3,64,64,64]{3,2,1,0:T(8,128)}, s32[]{:T(128)}) %tuple.73), condition=%wide.while_cond.1, body=%wide.while_body.1.sunk | while | flops 2 | bytes 4196993 | solution.py:116
  359.2 6.1 %dynamic-slice_dynamic-update-slice_fusion.5 = f32[3,64,64,64]{3,2,1,0:T(8,128)} fusion(f32[3,64,64,64]{3,2,1,0:T(8,128)} %get-tuple-element.218, s32[]{:T(128)} %get-tuple-element.215, f32[3,96,96,96]{3,2,1,0:T(8,128)} %get-tuple-element.221, s32[]{:T(128)} %bitcast.108, s32[]{:T(128)} %bitcast.109, s32[]{:T(128)} %bitcast.110, s32[]{:T(128)} %bitcast.111), kind=kLoop, calls=%fused_computation.4.clone.1 | loop fusion | bytes 4196864 | tf_op jit(solution)/shard_map/while/body/eval_jaxpr/vmap()/gather
  366.0 6.1 %dynamic-slice_dynamic-update-slice_fusion.5 = f32[3,64,64,64]{3,2,1,0:T(8,128)} fusion(f32[3,64,64,64]{3,2,1,0:T(8,128)} %get-tuple-element.218, s32[]{:T(128)} %get-tuple-element.215, f32[3,96,96,96]{3,2,1,0:T(8,128)} %get-tuple-element.221, s32[]{:T(128)} %bitcast.108, s32[]{:T(128)} %bitcast.109, s32[]{:T(128)} %bitcast.110, s32[]{:T(128)} %bitcast.111), kind=kLoop, calls=%fused_computation.4.clone.1 | loop fusion | bytes 4196864 | tf_op jit(solution)/shard_map/while/body/eval_jaxpr/vmap()/gather
  372.7 6.1 %dynamic-slice_dynamic-update-slice_fusion.5 = f32[3,64,64,64]{3,2,1,0:T(8,128)} fusion(f32[3,64,64,64]{3,2,1,0:T(8,128)} %get-tuple-element.218, s32[]{:T(128)} %get-tuple-element.215, f32[3,96,96,96]{3,2,1,0:T(8,128)} %get-tuple-element.221, s32[]{:T(128)} %bitcast.108, s32[]{:T(128)} %bitcast.109, s32[]{:T(128)} %bitcast.110, s32[]{:T(128)} %bitcast.111), kind=kLoop, calls=%fused_computation.4.clone.1 | loop fusion | bytes 4196864 | tf_op jit(solution)/shard_map/while/body/eval_jaxpr/vmap()/gather
  378.8 5.3 broadcast_in_dim.31
  384.1 11.9 %scatter_fusion = f32[5,64,64,64]{3,2,1,0:T(8,128)} fusion(f32[5,64,64,64]{3,2,1,0:T(8,128)} %broadcast_in_dim.31, s32[3]{0:T(128)S(1)} %fusion.77, f32[3,64,64,64]{3,2,1,0:T(8,128)} %get-tuple-element.38), kind=kCustom, calls=%fused_computation.1 | custom fusion | flops 786432 | bytes 9437196 | tf_op jit(solution)/shard_map/scatter-add | solution.py:182
  396.1 8.4 %slice.400 = f32[4,64,64,64]{3,2,1,0:T(8,128)} slice(f32[5,64,64,64]{3,2,1,0:T(8,128)} %scatter_fusion), slice={[1:5], [0:64], [0:64], [0:64]} | slice | bytes 8388608 | tf_op jit(solution)/shard_map/slice | solution.py:185
  404.5 7.4 %concatenate.27 = f32[4,64,32,128]{3,2,1,0:T(8,128)} reshape(f32[4,64,64,64]{3,2,1,0:T(8,128)} %slice.400) | data formatting | bytes 8388608 | tf_op jit(solution)/shard_map/concatenate | solution.py:185
  422.8 4.6 all_to_all.35
  427.4 9.7 %all-to-all-start.3 = ((f32[32,2,5,32,128]{4,3,1,2,0:T(8,128)}), f32[32,2,5,32,128]{4,3,1,2,0:T(8,128)}, u32[]{:S(2)}, u32[]{:S(2)}) async-start(f32[32,2,5,32,128]{4,3,1,2,0:T(8,128)} %copy.75), calls=%async_computation.3 | async-start | bytes 10485760 | tf_op jit(solution)/shard_map/all_to_all | solution.py:40
  437.2 120.5 %all-to-all-done.3 = f32[32,2,5,32,128]{4,3,1,2,0:T(8,128)} async-done(((f32[32,2,5,32,128]{4,3,1,2,0:T(8,128)}), f32[32,2,5,32,128]{4,3,1,2,0:T(8,128)}, u32[]{:S(2)}, u32[]{:S(2)}) %all-to-all-start.3) | async-done | bytes 5242912 | tf_op jit(solution)/shard_map/all_to_all | solution.py:40
  560.9 7.9 %all_to_all.36 = f32[32,2,5,32,128]{4,3,0,2,1:T(8,128)S(1)} all-to-all(f32[32,2,5,32,128]{4,3,0,2,1:T(8,128)S(1)} %copy.76), channel_id=1, replica_groups=mesh['orb'=4,'grid_0'=8,'grid_1'=4,'grid_2'=2] {'grid_2'}, dimensions={1} | all-to-all | bytes 10485760 | tf_op jit(solution)/shard_map/all_to_all | solution.py:40
  571.5 4.5 collective-permute-done.1
  (64 shorter events, 38.0 us)
Async XLA Ops:
  1.5 5.6 collective-permute-start
  7.3 14.6 %copy-start.5 = (s32[1,3,3]{2,0,1:T(1,128)S(1)}, s32[1,3,3]{2,0,1:T(1,128)}, u32[]{:S(2)}) copy-start(s32[1,3,3]{2,0,1:T(1,128)} %param.9) | copy-start | bytes 112
  7.4 15.0 %copy-start.6 = (s32[1,3]{1,0:T(1,128)S(1)}, s32[1,3]{1,0:T(1,128)}, u32[]{:S(2)}) copy-start(s32[1,3]{1,0:T(1,128)} %param.8) | copy-start | bytes 40
  7.4 2.3 copy-start.2
  9.8 130.8 %all-to-all-start = ((f32[320,32,128]{2,1,0:T(8,128)}), f32[320,32,128]{2,1,0:T(8,128)}, u32[]{:S(2)}, u32[]{:S(2)}) async-start(f32[320,32,128]{2,1,0:T(8,128)} %bitcast.114), calls=%async_computation | async-start | bytes 10485760 | tf_op jit(solution)/shard_map/all_to_all | solution.py:167
  254.8 167.9 %all-to-all-start.1 = ((f32[32,2,1,32,128]{4,3,1,2,0:T(8,128)}), f32[32,2,1,32,128]{4,3,1,2,0:T(8,128)S(1)}, u32[]{:S(2)}, u32[]{:S(2)}) async-start(f32[32,2,1,32,128]{4,3,1,2,0:T(8,128)} %reshape_transpose_reshape_reshape.3), calls=%async_computation.1 | async-start | bytes 2097152 | tf_op jit(solution)/shard_map/all_to_all | solution.py:40
  404.5 7.4 %copy-start.1 = (f32[64,64,64]{2,1,0:T(8,128)S(1)}, f32[64,64,64]{2,1,0:T(8,128)}, u32[]{:S(2)}) copy-start(f32[64,64,64]{2,1,0:T(8,128)} %get-tuple-element.97) | copy-start | bytes 3145732
  427.4 130.4 %all-to-all-start.3 = ((f32[32,2,5,32,128]{4,3,1,2,0:T(8,128)}), f32[32,2,5,32,128]{4,3,1,2,0:T(8,128)}, u32[]{:S(2)}, u32[]{:S(2)}) async-start(f32[32,2,5,32,128]{4,3,1,2,0:T(8,128)} %copy.75), calls=%async_computation.3 | async-start | bytes 10485760 | tf_op jit(solution)/shard_map/all_to_all | solution.py:40
  570.5 5.6 copy-start
  570.5 5.6 copy-start.3
  570.5 5.6 copy-start.4
  570.5 5.6 collective-permute-start.1
where the time goes:
time: 580 us; the launch traced here: 578 us
  waiting for transfers between devices  243 us (42%)
  other arithmetic  163 us (28%)
  local copies, waits for them, and re-layouts  128 us (22%)
  starting transfers between devices  30.4 us (5%)
  blocking collectives  12.5 us (2%)
    all_to_all x2, waiting for transfers between devices, exchange_in_order(): out = lax.all_to_all(out, axes[k], k, k, tiled=True)  121 us
    all_to_all x1, waiting for transfers between devices, local(): lax.all_to_all(windows, GRID, split_axis=0, concat_axis=1, tiled=True)  118 us
    add x2, other arithmetic, solve_potential(): direction = keep_weight * direction + residual_weight * residual  70.7 us
    reduce_sum x1, other arithmetic, pair_terms(): return (jnp.sum(own_terms, axis=0), partner_terms)  42.7 us
    gather x18, local copies, waits for them, and re-layouts  40.7 us
    pad x2, local copies, waits for them, and re-layouts, shift_box(): padded = jnp.pad(one_box, reach_cells)  21 us
    mul x1, other arithmetic, local(): -0.5 * apply_operator(own_boxes)  15.6 us
    all_to_all x2, starting transfers between devices, exchange_in_order(): out = lax.all_to_all(out, axes[k], k, k, tiled=True)  14.8 us
  transfers between devices with their start and end apart: 5, of which 3 were waited for; matrix products, arithmetic and copies ran while one was open for 29% of the time, Pallas kernels for 0%

commit v1 on v0

--- a/solution.py
+++ b/solution.py
@@ -164,7 +164,9 @@
     steps_ahead = -(-AHEAD // count_local)
     upper_rows = from_behind(orbitals[:AHEAD], "orb", -1)
     windows = build_windows(orbitals, upper_rows, count_local, steps_ahead)
-    widened = lax.all_to_all(windows, GRID, split_axis=0, concat_axis=1, tiled=True)
+    cells = jnp.split(windows, lax.axis_size(GRID), axis=0)
+    arrived = lax.all_to_all(jnp.stack(cells), GRID, 0, 0)
+    widened = jnp.concatenate(arrived, axis=1)
     full_rows = widened.shape[1]
     extended = widened.reshape(count_local + AHEAD, B, B, B)
     own_boxes = extended[:count_local]

time: 580 us -> 583 us (level)
    another operation x0 -> x1, local copies, waits for them, and re-layouts: none -> 8.53 us  [local(): extended = widened.reshape(count_local + AHEAD, B, B, B)]
    reshape x1 -> x0, local copies, waits for them, and re-layouts: 8.52 us -> none  [local(): extended = widened.reshape(count_local + AHEAD, B, B, B)]
    unnamed x25 -> x23, local copies, waits for them, and re-layouts: 13 us -> 14.9 us
where the time goes in v1:
time: 583 us; the launch traced here: 581 us
  waiting for transfers between devices  243 us (42%)
  other arithmetic  163 us (28%)
  local copies, waits for them, and re-layouts  131 us (22%)
  starting transfers between devices  30.1 us (5%)
  blocking collectives  12.5 us (2%)
    all_to_all x2, waiting for transfers between devices, exchange_in_order(): out = lax.all_to_all(out, axes[k], k, k, tiled=True)  121 us
    all_to_all x1, waiting for transfers between devices, local(): arrived = lax.all_to_all(jnp.stack(cells), GRID, 0, 0)  118 us
    add x2, other arithmetic, solve_potential(): direction = keep_weight * direction + residual_weight * residual  70.9 us
    reduce_sum x1, other arithmetic, pair_terms(): return (jnp.sum(own_terms, axis=0), partner_terms)  42.6 us
    gather x18, local copies, waits for them, and re-layouts  40.7 us
    pad x2, local copies, waits for them, and re-layouts, shift_box(): padded = jnp.pad(one_box, reach_cells)  21 us
    mul x1, other arithmetic, local(): -0.5 * apply_operator(own_boxes)  15.6 us
    unnamed x23, local copies, waits for them, and re-layouts  14.9 us
  transfers between devices with their start and end apart: 5, of which 3 were waited for; matrix products, arithmetic and copies ran while one was open for 29% of the time, Pallas kernels for 0%

profile of v1, /device:TPU:2, one launch (start us, length us, event | category | flops | bytes accessed | tf_op | source)
XLA Modules:
  0.0 580.9 jit_solution(7266696677688296137)
XLA Ops:
  12.6 12.2 %all-to-all-start = ((f32[64,5,32,128]{3,2,1,0:T(8,128)}), f32[64,5,32,128]{3,2,1,0:T(8,128)}, u32[]{:S(2)}, u32[]{:S(2)}) async-start(f32[64,5,32,128]{3,2,1,0:T(8,128)} %fusion.64), calls=%async_computation | async-start | bytes 10485760 | tf_op jit(solution)/shard_map/all_to_all | solution.py:168
  25.2 118.1 %all-to-all-done = f32[64,5,32,128]{3,2,1,0:T(8,128)} async-done(((f32[64,5,32,128]{3,2,1,0:T(8,128)}), f32[64,5,32,128]{3,2,1,0:T(8,128)}, u32[]{:S(2)}, u32[]{:S(2)}) %all-to-all-start) | async-done | bytes 5242912 | tf_op jit(solution)/shard_map/all_to_all | solution.py:168
  143.4 8.5 %reshape_reshape.8 = f32[5,64,64,64]{3,2,0,1:T(8,128)} reshape(f32[5,64,32,128]{3,2,0,1:T(8,128)} %bitcast.8) | data formatting | bytes 10485760 | tf_op jit(solution)/shard_map/reshape;reshape | solution.py:171
  155.3 7.5 %gather_fusion = f32[3,64,64,64]{3,2,1,0:T(8,128)} fusion(f32[5,64,64,64]{3,2,0,1:T(8,128)} %reshape_reshape.8, s32[1024]{0:T(1024)S(1)} %pad_clamp_fusion), kind=kCustom, calls=%fused_computation | custom fusion | bytes 6291468 | tf_op jit(solution)/shard_map/while/body/eval_jaxpr/gather | solution.py:178
  162.8 10.5 %pad.51 = f32[3,96,96,96]{3,2,1,0:T(8,128)} pad(f32[3,64,64,64]{3,2,1,0:T(8,128)} %gather_fusion, f32[]{:T(128)} %constant.49.clone.1), padding=0_0x16_16x16_16x16_16 | pad | bytes 13762564 | tf_op jit(solution)/shard_map/while/body/eval_jaxpr/vmap(jit(_pad))/pad | solution.py:114
  173.3 3.5 broadcast.154.clone
  176.8 20.5 %while.2 = (s32[]{:T(128)}, f32[3,96,96,96]{3,2,1,0:T(8,128)}, s32[3,4]{1,0:T(4,128)S(1)}, f32[3,64,64,64]{3,2,1,0:T(8,128)}, s32[]{:T(128)}) while((s32[]{:T(128)}, f32[3,96,96,96]{3,2,1,0:T(8,128)}, s32[3,4]{1,0:T(4,128)S(1)}, f32[3,64,64,64]{3,2,1,0:T(8,128)}, s32[]{:T(128)}) %tuple.68), condition=%wide.while_cond, body=%wide.while_body.sunk | while | flops 2 | bytes 4196993 | solution.py:116
  177.4 6.2 %dynamic-slice_dynamic-update-slice_fusion.4 = f32[3,64,64,64]{3,2,1,0:T(8,128)} fusion(f32[3,64,64,64]{3,2,1,0:T(8,128)} %get-tuple-element.195, s32[]{:T(128)} %get-tuple-element.192, f32[3,96,96,96]{3,2,1,0:T(8,128)} %get-tuple-element.198, s32[]{:T(128)} %bitcast.101, s32[]{:T(128)} %bitcast.102, s32[]{:T(128)} %bitcast.103, s32[]{:T(128)} %bitcast.104), kind=kLoop, calls=%fused_computation.2.clone.1 | loop fusion | bytes 4196864 | tf_op jit(solution)/shard_map/while/body/eval_jaxpr/vmap()/gather
  184.3 6.1 %dynamic-slice_dynamic-update-slice_fusion.4 = f32[3,64,64,64]{3,2,1,0:T(8,128)} fusion(f32[3,64,64,64]{3,2,1,0:T(8,128)} %get-tuple-element.195, s32[]{:T(128)} %get-tuple-element.192, f32[3,96,96,96]{3,2,1,0:T(8,128)} %get-tuple-element.198, s32[]{:T(128)} %bitcast.101, s32[]{:T(128)} %bitcast.102, s32[]{:T(128)} %bitcast.103, s32[]{:T(128)} %bitcast.104), kind=kLoop, calls=%fused_computation.2.clone.1 | loop fusion | bytes 4196864 | tf_op jit(solution)/shard_map/while/body/eval_jaxpr/vmap()/gather
  191.1 6.2 %dynamic-slice_dynamic-update-slice_fusion.4 = f32[3,64,64,64]{3,2,1,0:T(8,128)} fusion(f32[3,64,64,64]{3,2,1,0:T(8,128)} %get-tuple-element.195, s32[]{:T(128)} %get-tuple-element.192, f32[3,96,96,96]{3,2,1,0:T(8,128)} %get-tuple-element.198, s32[]{:T(128)} %bitcast.101, s32[]{:T(128)} %bitcast.102, s32[]{:T(128)} %bitcast.103, s32[]{:T(128)} %bitcast.104), kind=kLoop, calls=%fused_computation.2.clone.1 | loop fusion | bytes 4196864 | tf_op jit(solution)/shard_map/while/body/eval_jaxpr/vmap()/gather
  197.2 6.9 %multiply_multiply_fusion = f32[3,64,64,64]{3,2,1,0:T(8,128)} fusion(f32[3,64,64,64]{3,2,1,0:T(8,128)} %get-tuple-element.30, f32[64,64,64]{2,1,0:T(8,128)S(1)} %mul.171), kind=kLoop, calls=%fused_computation.93 | loop fusion | flops 1572864 | bytes 7340032 | tf_op jit(solution)/shard_map/while/body/eval_jaxpr/vmap()/div | solution.py:100
  204.1 35.3 %multiply_add_fusion.1 = (f32[3,64,64,64]{3,2,1,0:T(8,128)}, f32[3,64,64,64]{3,2,1,0:T(8,128)}) fusion(f32[3,64,64,64]{3,2,1,0:T(8,128)} %get-tuple-element.30, f32[64,64,64]{2,1,0:T(8,128)S(1)} %mul.171, f32[3,64,64,64]{3,2,1,0:T(8,128)} %multiply_multiply_fusion), kind=kLoop, calls=%fused_computation.92 | loop fusion | flops 16515072 | bytes 13631488 | tf_op jit(solution)/shard_map/while/body/eval_jaxpr/vmap()/add | solution.py:107
  239.4 15.6 %fusion.56 = f32[1,64,64,64]{3,2,1,0:T(8,128)} fusion(f32[1,64,64,64]{3,2,1,0:T(8,128)} %slice.355), kind=kLoop, calls=%fused_computation.116 | loop fusion | flops 4194304 | bytes 2097152 | tf_op jit(solution)/shard_map/mul | solution.py:186
  257.6 5.1 all-to-all-start.1
  262.6 35.6 %multiply_add_fusion = (f32[3,64,64,64]{3,2,1,0:T(8,128)}, f32[3,64,64,64]{3,2,1,0:T(8,128)}) fusion(f32[3,64,64,64]{3,2,1,0:T(8,128)} %get-tuple-element.93, f32[3,64,64,64]{3,2,1,0:T(8,128)} %get-tuple-element.94), kind=kLoop, calls=%fused_computation.91 | loop fusion | flops 14942208 | bytes 12582912 | tf_op jit(solution)/shard_map/while/body/eval_jaxpr/vmap()/add | solution.py:107
  298.3 42.6 %multiply_reduce_fusion = (f32[64,64,64]{2,1,0:T(8,128)}, f32[3,64,64,64]{3,2,1,0:T(8,128)}) fusion(f32[3,64,64,64]{3,2,1,0:T(8,128)} %get-tuple-element.30, f32[3,64,64,64]{3,2,1,0:T(8,128)} %get-tuple-element.92, f32[3,64,64,64]{3,2,1,0:T(8,128)} %get-tuple-element.91, f32[3,64,64,64]{3,2,1,0:T(8,128)} %get-tuple-element.93, f32[64,64,64]{2,1,0:T(8,128)S(1)} %mul.171), kind=kLoop, calls=%fused_computation.90 | loop fusion | flops 20185088 | bytes 17825792 | tf_op jit(solution)/shard_map/while/body/eval_jaxpr/reduce_sum | solution.py:127
  340.9 6.8 %broadcast_multiply_fusion = f32[3,64,64,64]{3,2,1,0:T(8,128)} fusion(f32[3,64,64,64]{3,2,1,0:T(8,128)} %get-tuple-element.90, f32[64,64,64]{2,1,0:T(8,128)S(1)} %mul.171), kind=kLoop, calls=%fused_computation.95 | loop fusion | flops 786432 | bytes 7340032 | tf_op jit(solution)/shard_map/while/body/eval_jaxpr/vmap()/mul | solution.py:124
  347.6 10.5 %pad.55 = f32[3,96,96,96]{3,2,1,0:T(8,128)} pad(f32[3,64,64,64]{3,2,1,0:T(8,128)} %broadcast_multiply_fusion, f32[]{:T(128)} %constant.49.clone.1), padding=0_0x16_16x16_16x16_16 | pad | bytes 13762564 | tf_op jit(solution)/shard_map/while/body/eval_jaxpr/vmap(jit(_pad))/pad | solution.py:114
  358.1 3.4 broadcast.154
  361.5 20.2 %while.3 = (s32[]{:T(128)}, f32[3,96,96,96]{3,2,1,0:T(8,128)}, s32[3,4]{1,0:T(4,128)S(1)}, f32[3,64,64,64]{3,2,1,0:T(8,128)}, s32[]{:T(128)}) while((s32[]{:T(128)}, f32[3,96,96,96]{3,2,1,0:T(8,128)}, s32[3,4]{1,0:T(4,128)S(1)}, f32[3,64,64,64]{3,2,1,0:T(8,128)}, s32[]{:T(128)}) %tuple.71), condition=%wide.while_cond.1, body=%wide.while_body.1.sunk | while | flops 2 | bytes 4196993 | solution.py:116
  362.1 6.1 %dynamic-slice_dynamic-update-slice_fusion.5 = f32[3,64,64,64]{3,2,1,0:T(8,128)} fusion(f32[3,64,64,64]{3,2,1,0:T(8,128)} %get-tuple-element.210, s32[]{:T(128)} %get-tuple-element.207, f32[3,96,96,96]{3,2,1,0:T(8,128)} %get-tuple-element.213, s32[]{:T(128)} %bitcast.105, s32[]{:T(128)} %bitcast.106, s32[]{:T(128)} %bitcast.107, s32[]{:T(128)} %bitcast.108), kind=kLoop, calls=%fused_computation.4.clone.1 | loop fusion | bytes 4196864 | tf_op jit(solution)/shard_map/while/body/eval_jaxpr/vmap()/gather
  368.9 6.1 %dynamic-slice_dynamic-update-slice_fusion.5 = f32[3,64,64,64]{3,2,1,0:T(8,128)} fusion(f32[3,64,64,64]{3,2,1,0:T(8,128)} %get-tuple-element.210, s32[]{:T(128)} %get-tuple-element.207, f32[3,96,96,96]{3,2,1,0:T(8,128)} %get-tuple-element.213, s32[]{:T(128)} %bitcast.105, s32[]{:T(128)} %bitcast.106, s32[]{:T(128)} %bitcast.107, s32[]{:T(128)} %bitcast.108), kind=kLoop, calls=%fused_computation.4.clone.1 | loop fusion | bytes 4196864 | tf_op jit(solution)/shard_map/while/body/eval_jaxpr/vmap()/gather
  375.7 6.1 %dynamic-slice_dynamic-update-slice_fusion.5 = f32[3,64,64,64]{3,2,1,0:T(8,128)} fusion(f32[3,64,64,64]{3,2,1,0:T(8,128)} %get-tuple-element.210, s32[]{:T(128)} %get-tuple-element.207, f32[3,96,96,96]{3,2,1,0:T(8,128)} %get-tuple-element.213, s32[]{:T(128)} %bitcast.105, s32[]{:T(128)} %bitcast.106, s32[]{:T(128)} %bitcast.107, s32[]{:T(128)} %bitcast.108), kind=kLoop, calls=%fused_computation.4.clone.1 | loop fusion | bytes 4196864 | tf_op jit(solution)/shard_map/while/body/eval_jaxpr/vmap()/gather
  381.7 5.3 broadcast_in_dim.31
  387.1 11.9 %scatter_fusion = f32[5,64,64,64]{3,2,1,0:T(8,128)} fusion(f32[5,64,64,64]{3,2,1,0:T(8,128)} %broadcast_in_dim.31, s32[3]{0:T(128)S(1)} %fusion.77, f32[3,64,64,64]{3,2,1,0:T(8,128)} %get-tuple-element.38), kind=kCustom, calls=%fused_computation.1 | custom fusion | flops 786432 | bytes 9437196 | tf_op jit(solution)/shard_map/scatter-add | solution.py:184
  399.0 8.4 %slice.465 = f32[4,64,64,64]{3,2,1,0:T(8,128)} slice(f32[5,64,64,64]{3,2,1,0:T(8,128)} %scatter_fusion), slice={[1:5], [0:64], [0:64], [0:64]} | slice | bytes 8388608 | tf_op jit(solution)/shard_map/slice | solution.py:187
  407.4 7.4 %concatenate.27 = f32[4,64,32,128]{3,2,1,0:T(8,128)} reshape(f32[4,64,64,64]{3,2,1,0:T(8,128)} %slice.465) | data formatting | bytes 8388608 | tf_op jit(solution)/shard_map/concatenate | solution.py:187
  425.8 4.6 all_to_all.25
  430.4 9.8 %all-to-all-start.3 = ((f32[32,2,5,32,128]{4,3,1,2,0:T(8,128)}), f32[32,2,5,32,128]{4,3,1,2,0:T(8,128)}, u32[]{:S(2)}, u32[]{:S(2)}) async-start(f32[32,2,5,32,128]{4,3,1,2,0:T(8,128)} %copy.64), calls=%async_computation.3 | async-start | bytes 10485760 | tf_op jit(solution)/shard_map/all_to_all | solution.py:40
  440.2 120.5 %all-to-all-done.3 = f32[32,2,5,32,128]{4,3,1,2,0:T(8,128)} async-done(((f32[32,2,5,32,128]{4,3,1,2,0:T(8,128)}), f32[32,2,5,32,128]{4,3,1,2,0:T(8,128)}, u32[]{:S(2)}, u32[]{:S(2)}) %all-to-all-start.3) | async-done | bytes 5242912 | tf_op jit(solution)/shard_map/all_to_all | solution.py:40
  563.9 7.9 %all_to_all.26 = f32[32,2,5,32,128]{4,3,0,2,1:T(8,128)S(1)} all-to-all(f32[32,2,5,32,128]{4,3,0,2,1:T(8,128)S(1)} %copy.65), channel_id=1, replica_groups=mesh['orb'=4,'grid_0'=8,'grid_1'=4,'grid_2'=2] {'grid_2'}, dimensions={1} | all-to-all | bytes 10485760 | tf_op jit(solution)/shard_map/all_to_all | solution.py:40
  574.3 4.8 collective-permute-done.1
  (62 shorter events, 40.5 us)
Async XLA Ops:
  1.5 6.7 %collective-permute-start = (f32[4,32,128]{2,1,0:T(8,128)S(1)}, f32[4,32,128]{2,1,0:T(8,128)S(1)}, u32[]{:S(2)}, u32[]{:S(2)}) collective-permute-start(f32[4,32,128]{2,1,0:T(8,128)S(1)} %slice.345), channel_id=1, source_target_pairs={{0,192},{64,0},{128,64},{192,128},{1,193},{65,1},{129,65},{193,129... | collective-permute-start | bytes 196616 | tf_op jit(solution)/shard_map/ppermute | solution.py:22
  11.5 13.3 %copy-start.4 = (s32[1,3,3]{2,0,1:T(1,128)S(1)}, s32[1,3,3]{2,0,1:T(1,128)}, u32[]{:S(2)}) copy-start(s32[1,3,3]{2,0,1:T(1,128)} %param.9) | copy-start | bytes 112
  11.5 13.7 %copy-start.5 = (s32[1,3]{1,0:T(1,128)S(1)}, s32[1,3]{1,0:T(1,128)}, u32[]{:S(2)}) copy-start(s32[1,3]{1,0:T(1,128)} %param.8) | copy-start | bytes 40
  12.6 130.8 %all-to-all-start = ((f32[64,5,32,128]{3,2,1,0:T(8,128)}), f32[64,5,32,128]{3,2,1,0:T(8,128)}, u32[]{:S(2)}, u32[]{:S(2)}) async-start(f32[64,5,32,128]{3,2,1,0:T(8,128)} %fusion.64), calls=%async_computation | async-start | bytes 10485760 | tf_op jit(solution)/shard_map/all_to_all | solution.py:168
  257.6 168.2 %all-to-all-start.1 = ((f32[32,2,1,32,128]{4,3,1,2,0:T(8,128)}), f32[32,2,1,32,128]{4,3,1,2,0:T(8,128)S(1)}, u32[]{:S(2)}, u32[]{:S(2)}) async-start(f32[32,2,1,32,128]{4,3,1,2,0:T(8,128)} %reshape_transpose_reshape_reshape.3), calls=%async_computation.1 | async-start | bytes 2097152 | tf_op jit(solution)/shard_map/all_to_all | solution.py:40
  407.4 7.4 %copy-start.1 = (f32[64,64,64]{2,1,0:T(8,128)S(1)}, f32[64,64,64]{2,1,0:T(8,128)}, u32[]{:S(2)}) copy-start(f32[64,64,64]{2,1,0:T(8,128)} %get-tuple-element.89) | copy-start | bytes 3145732
  430.4 130.4 %all-to-all-start.3 = ((f32[32,2,5,32,128]{4,3,1,2,0:T(8,128)}), f32[32,2,5,32,128]{4,3,1,2,0:T(8,128)}, u32[]{:S(2)}, u32[]{:S(2)}) async-start(f32[32,2,5,32,128]{4,3,1,2,0:T(8,128)} %copy.64), calls=%async_computation.3 | async-start | bytes 10485760 | tf_op jit(solution)/shard_map/all_to_all | solution.py:40
  573.5 5.6 copy-start
  573.5 5.6 copy-start.2
  573.5 5.6 copy-start.3
  573.5 5.6 collective-permute-start.1
